TPU v7x, 32 devices: a whole 2x2x4 slice. The times are simulated.
32 devices in a mesh: grp: 8 (over y, x, core), wide: 4 (over z).
Axes of the slice: x: 2, y: 2, z: 4, core: 2. Of those that a mesh axis runs over, the one named last changes fastest.
Arguments:
- gradient: bfloat16 [8, 4, 16, 4096], P('grp', 'wide'), may hold values from -6 to 6
- residual: float32 [8, 4, 16, 4096], P('grp', 'wide'), may hold values from -4 to 4
- selected: int32 [8, 4, 4, 32], P('grp', 'wide'), may hold values from 0 to 127, as said below
- counts: int32 [8, 4, 4], P('grp', 'wide'), may hold values from 1 to 32, as said below
Outputs:
- update: float32 [4, 4, 4096], P('wide')
- new_residual: float32 [8, 4, 16, 4096], P('grp', 'wide')
Inputs may be any that keep to these rules, and one draw needn't show every extreme that they name: `selected`: for each device and shard, 32 distinct block numbers of that shard; entries at or past the count are ignored. `counts`: one shard has 32 on every device; every device has at most one other shard at 32, the rest at most 16.
All inputs are finite; a program needn't handle non-finite values.
Results may differ from a plain program's by a relative error of at most 0.0003.
Values sent between devices are 32-bit elements; how exact they have to be, the bound alone decides.
No kernel may reach another device: no remote copies, remote signals or barrier semaphores. Data moves between devices by JAX's collectives and lax.ppermute only.
A program may use at most 64 MiB of HBM per device.

v0:
```python
import jax
import jax.numpy as jnp
from jax import lax
from jax.sharding import PartitionSpec as P


def body(gradient, residual, selected, counts):
    shards = lax.axis_size("wide")
    groups = lax.axis_size("grp")
    rows = gradient.shape[2]
    width = gradient.shape[3]
    block_len = 128
    own_rows = rows // shards
    own_blocks = own_rows * width // block_len
    slots = selected.shape[3]
    accumulated = gradient[0, 0].astype(jnp.float32) + residual[0, 0]
    blocks = accumulated.reshape(shards, own_blocks, block_len)
    picks = selected[0, 0]
    used = counts[0, 0]
    block_ids = jnp.arange(own_blocks, dtype=jnp.int32)
    one_hot = (picks[:, :, None] == block_ids).astype(jnp.float32)
    valid = (jnp.arange(slots, dtype=jnp.int32)[None, :] < used[:, None]).astype(jnp.float32)
    mask = jnp.einsum("wk,wkb->wb", valid, one_hot, precision=lax.Precision.HIGHEST)
    new_residual = (blocks * (1.0 - mask[..., None])).reshape(1, 1, rows, width)
    chosen = (
        jnp.einsum("wkb,wbc->wkc", one_hot, blocks, precision=lax.Precision.HIGHEST)
        * valid[..., None]
    )
    chosen_ids = picks.astype(jnp.float32)
    arrived, arrived_ids = (
        lax.all_to_all(chosen, "wide", split_axis=0, concat_axis=0, tiled=True),
        lax.all_to_all(chosen_ids, "wide", split_axis=0, concat_axis=0, tiled=True),
    )
    arrived_hot = (arrived_ids[:, :, None] == block_ids.astype(jnp.float32)).astype(jnp.float32)
    partial_sum = jnp.einsum("skb,skc->bc", arrived_hot, arrived, precision=lax.Precision.HIGHEST)
    summed = lax.psum(partial_sum, "grp")
    update = (summed / groups).reshape(1, own_rows, width)
    return (update, new_residual)


def solution(mesh):
    return jax.shard_map(
        body,
        mesh=mesh,
        in_specs=(
            P("grp", "wide", None, None),
            P("grp", "wide", None, None),
            P("grp", "wide", None, None),
            P("grp", "wide", None),
        ),
        out_specs=(P("wide", None, None), P("grp", "wide", None, None)),
        check_vma=False,
    )
```

profile of v0, /device:TPU:0, one launch (start us, length us, event | category | flops | bytes accessed | tf_op | source)
XLA Modules:
  0.0 91.7 jit_solution(3083365458631421438)
XLA Ops:
  7.2 1.3 %convert_element_type.35 = f32[1,1,4,32]{3,2,1,0:T(4,128)} convert(s32[1,1,4,32]{3,2,1,0:T(4,128)} %param.6) | non-fusion elementwise | flops 128 | bytes 1024 | tf_op jit(solution)/shard_map/convert_element_type | solution.py:29
  8.4 6.3 %all-to-all-start = ((f32[4,1,32]{2,1,0:T(1,128)}), f32[4,1,32]{2,1,0:T(1,128)S(1)}, u32[]{:S(2)}, u32[]{:S(2)}) async-start(f32[4,1,32]{2,1,0:T(1,128)} %bitcast.1), calls=%async_computation | async-start | bytes 4096 | tf_op jit(solution)/shard_map/all_to_all | solution.py:32
  14.8 0.0 copy-start.3
  14.8 0.7 copy-done.3
  15.4 0.1 fusion.8
  15.5 0.0 copy-start.2
  15.5 0.7 copy-done.2
  16.2 0.2 fusion
  16.4 0.1 mul.21
  16.5 0.0 copy-start
  16.5 0.0 copy-start.1
  16.5 0.1 mul.22
  16.6 0.9 copy-done
  17.5 0.0 copy-done.1
  17.5 0.7 fusion.9
  18.3 0.9 convolution_multiply_fusion
  19.2 1.1 %all-to-all-done = f32[4,1,32]{2,1,0:T(1,128)S(1)} async-done(((f32[4,1,32]{2,1,0:T(1,128)}), f32[4,1,32]{2,1,0:T(1,128)S(1)}, u32[]{:S(2)}, u32[]{:S(2)}) %all-to-all-start) | async-done | bytes 544 | tf_op jit(solution)/shard_map/all_to_all | solution.py:32
  20.3 4.0 %all-to-all-start.1 = ((f32[4,32,128]{2,1,0:T(8,128)}), f32[4,32,128]{2,1,0:T(8,128)S(1)}, u32[]{:S(2)}, u32[]{:S(2)}) async-start(f32[4,32,128]{2,1,0:T(8,128)} %convolution_multiply_fusion), calls=%async_computation.1 | async-start | bytes 131072 | tf_op jit(solution)/shard_map/all_to_all | solution.py:31
  24.3 0.0 all-reduce.2.cloned.1.call-start
  24.3 5.7 %all-to-all-done.1 = f32[4,32,128]{2,1,0:T(8,128)S(1)} async-done(((f32[4,32,128]{2,1,0:T(8,128)}), f32[4,32,128]{2,1,0:T(8,128)S(1)}, u32[]{:S(2)}, u32[]{:S(2)}) %all-to-all-start.1) | async-done | bytes 65568 | tf_op jit(solution)/shard_map/all_to_all | solution.py:31
  30.1 0.9 %convolution_bitcast_fusion = f32[128,128]{1,0:T(8,128)} fusion(f32[4,32,128]{2,1,0:T(8,128)S(1)} %all-to-all-done.1, f32[128]{0:T(128)S(1)} %iota_convert_fusion, f32[4,32]{1,0:T(4,128)S(1)} %bitcast.16), kind=kOutput, calls=%fused_computation | convolution fusion | flops 25182208 | bytes 132096 | tf_op jit(solution)/shard_map/skb,skc->bc/dot_general | solution.py:35
  31.0 0.0 all-reduce.2.cloned.1.call-update
  31.0 52.4 %all-reduce.2.cloned.1.call-done = f32[128,128]{1,0:T(8,128)} async-done(((f32[128,128]{1,0:T(8,128)}), f32[128,128]{1,0:T(8,128)}) %all-reduce.2.cloned.1.call-update) | async-done | bytes 65552 | tf_op jit(solution)/shard_map/psum | solution.py:36
  83.4 0.8 broadcast_multiply_fusion
  84.2 0.7 reshape.63
  (3 shorter events, 0.1 us)
Async XLA Ops:
  8.4 11.9 %all-to-all-start = ((f32[4,1,32]{2,1,0:T(1,128)}), f32[4,1,32]{2,1,0:T(1,128)S(1)}, u32[]{:S(2)}, u32[]{:S(2)}) async-start(f32[4,1,32]{2,1,0:T(1,128)} %bitcast.1), calls=%async_computation | async-start | bytes 4096 | tf_op jit(solution)/shard_map/all_to_all | solution.py:32
  14.8 0.7 copy-start.3
  15.5 0.7 copy-start.2
  16.5 1.0 %copy-start = (f32[1,1,16,4096]{3,2,1,0:T(8,128)S(1)}, f32[1,1,16,4096]{3,2,1,0:T(8,128)}, u32[]{:S(2)}) copy-start(f32[1,1,16,4096]{3,2,1,0:T(8,128)} %param.5) | copy-start | bytes 786436
  16.5 1.0 %copy-start.1 = (bf16[1,1,16,4096]{3,2,1,0:T(8,128)(2,1)S(1)}, bf16[1,1,16,4096]{3,2,1,0:T(8,128)(2,1)}, u32[]{:S(2)}) copy-start(bf16[1,1,16,4096]{3,2,1,0:T(8,128)(2,1)} %param.4) | copy-start | bytes 393220
  20.3 9.7 %all-to-all-start.1 = ((f32[4,32,128]{2,1,0:T(8,128)}), f32[4,32,128]{2,1,0:T(8,128)S(1)}, u32[]{:S(2)}, u32[]{:S(2)}) async-start(f32[4,32,128]{2,1,0:T(8,128)} %convolution_multiply_fusion), calls=%async_computation.1 | async-start | bytes 131072 | tf_op jit(solution)/shard_map/all_to_all | solution.py:31
  24.3 59.1 %all-reduce.2.cloned.1.call-start = ((), (), s32[]{:S(2)}) async-start(), calls=%async_computation.2 | async-start | bytes 131072 | tf_op jit(solution)/shard_map/psum | solution.py:36
Sparse Core Ops, SparseCore 0:
  31.1 52.2 all-reduce.1
where the time goes:
time: 92.1 us; the launch traced here: 91.7 us
  waiting for transfers between devices  59.3 us (64%)
  between operations  14.1 us (15%)
  starting transfers between devices  10.3 us (11%)
  local copies, waits for them, and re-layouts  3.13 us (3%)
  other arithmetic  2.93 us (3%)
  matrix products  2.05 us (2%)
    psum x1, waiting for transfers between devices, body(): summed = lax.psum(partial_sum, 'grp')  52.4 us
    all_to_all x1, starting transfers between devices, body(): lax.all_to_all(chosen_ids, 'wide', split_axis=0, concat_axis=0, tiled=True)  6.35 us
    all_to_all x1, waiting for transfers between devices, body(): lax.all_to_all(chosen, 'wide', split_axis=0, concat_axis=0, tiled=True)  5.74 us
    all_to_all x1, starting transfers between devices, body(): lax.all_to_all(chosen, 'wide', split_axis=0, concat_axis=0, tiled=True)  3.96 us
    unnamed x8, local copies, waits for them, and re-layouts  2.25 us
  transfers between devices with their start and end apart: 3, of which 3 were waited for; matrix products, arithmetic and copies ran while one was open for 2% of the time, Pallas kernels for 0%

commit v1 on v0

--- a/solution.py
+++ b/solution.py
@@ -33,7 +33,7 @@
     )
     arrived_hot = (arrived_ids[:, :, None] == block_ids.astype(jnp.float32)).astype(jnp.float32)
     partial_sum = jnp.einsum("skb,skc->bc", arrived_hot, arrived, precision=lax.Precision.HIGHEST)
-    summed = lax.psum(partial_sum, "grp")
+    summed = jnp.sum(lax.all_gather(partial_sum, "grp"), axis=0)
     update = (summed / groups).reshape(1, own_rows, width)
     return (update, new_residual)
 

time: 92.1 us -> 34.8 us (0.38)
  waiting for transfers between devices: 59.3 us -> 6.87 us
  between operations: 14.1 us -> 0.68 us
  blocking collectives: 0 us -> 9.86 us
    psum x1 -> x0, waiting for transfers between devices: 52.4 us -> none  [body(): summed = lax.psum(partial_sum, 'grp')]
    all_gather x0 -> x1, blocking collectives: none -> 9.86 us  [body(): summed = jnp.sum(lax.all_gather(partial_sum, 'grp'), axis=0)]
  transfers between devices with their start and end apart: 3 -> 2, of which waited for: 3 -> 2; matrix products, arithmetic and copies ran while one was open for 2% -> 6% of each run, Pallas kernels for 0% -> 0%
where the time goes in v1:
time: 34.8 us; the launch traced here: 34.4 us
  starting transfers between devices  10.3 us (30%)
  blocking collectives  9.86 us (28%)
  waiting for transfers between devices  6.87 us (20%)
  local copies, waits for them, and re-layouts  3.13 us (9%)
  other arithmetic  2.13 us (6%)
  matrix products  1.42 us (4%)
  between operations  0.68 us (2%)
    all_gather x1, blocking collectives, body(): summed = jnp.sum(lax.all_gather(partial_sum, 'grp'), axis=0)  9.86 us
    all_to_all x1, starting transfers between devices, body(): lax.all_to_all(chosen_ids, 'wide', split_axis=0, concat_axis=0, tiled=True)  6.35 us
    all_to_all x1, waiting for transfers between devices, body(): lax.all_to_all(chosen, 'wide', split_axis=0, concat_axis=0, tiled=True)  5.74 us
    all_to_all x1, starting transfers between devices, body(): lax.all_to_all(chosen, 'wide', split_axis=0, concat_axis=0, tiled=True)  3.96 us
    unnamed x8, local copies, waits for them, and re-layouts  2.25 us
    convert_element_type x1, other arithmetic, body(): chosen_ids = picks.astype(jnp.float32)  1.27 us
    all_to_all x1, waiting for transfers between devices, body(): lax.all_to_all(chosen_ids, 'wide', split_axis=0, concat_axis=0, tiled=True)  1.13 us
    dot_general x1, matrix products, body(): jnp.einsum('wkb,wbc->wkc', one_hot, blocks, precision=lax.Precision.HIGHEST)  0.91 us
  transfers between devices with their start and end apart: 2, of which 2 were waited for; matrix products, arithmetic and copies ran while one was open for 6% of the time, Pallas kernels for 0%

profile of v1, /device:TPU:0, one launch (start us, length us, event | category | flops | bytes accessed | tf_op | source)
XLA Modules:
  0.0 34.4 jit_solution(12081509573842560310)
XLA Ops:
  0.6 1.3 %convert_element_type.35 = f32[1,1,4,32]{3,2,1,0:T(4,128)} convert(s32[1,1,4,32]{3,2,1,0:T(4,128)} %param.6) | non-fusion elementwise | flops 128 | bytes 1024 | tf_op jit(solution)/shard_map/convert_element_type | solution.py:29
  1.9 6.3 %all-to-all-start = ((f32[4,1,32]{2,1,0:T(1,128)}), f32[4,1,32]{2,1,0:T(1,128)S(1)}, u32[]{:S(2)}, u32[]{:S(2)}) async-start(f32[4,1,32]{2,1,0:T(1,128)} %bitcast.1), calls=%async_computation | async-start | bytes 4096 | tf_op jit(solution)/shard_map/all_to_all | solution.py:32
  8.2 0.0 copy-start.3
  8.2 0.7 %copy-done.3 = s32[1,1,4]{2,1,0:T(1,128)S(1)} copy-done((s32[1,1,4]{2,1,0:T(1,128)S(1)}, s32[1,1,4]{2,1,0:T(1,128)}, u32[]{:S(2)}) %copy-start.3) | copy-done | bytes 40
  8.9 0.1 fusion.8
  9.0 0.0 copy-start.2
  9.0 0.7 %copy-done.2 = s32[1,1,4,32]{3,2,1,0:T(4,128)S(1)} copy-done((s32[1,1,4,32]{3,2,1,0:T(4,128)S(1)}, s32[1,1,4,32]{3,2,1,0:T(4,128)}, u32[]{:S(2)}) %copy-start.2) | copy-done | bytes 536
  9.7 0.2 fusion
  9.9 0.1 mul.21
  10.0 0.0 copy-start
  10.0 0.0 copy-start.1
  10.0 0.1 mul.22
  10.1 0.9 %copy-done = f32[1,1,16,4096]{3,2,1,0:T(8,128)S(1)} copy-done((f32[1,1,16,4096]{3,2,1,0:T(8,128)S(1)}, f32[1,1,16,4096]{3,2,1,0:T(8,128)}, u32[]{:S(2)}) %copy-start) | copy-done | bytes 262168
  11.0 0.0 copy-done.1
  11.0 0.7 %fusion.9 = (f32[1,1,16,4096]{3,2,1,0:T(8,128)}, f32[1,1,16,4096]{3,2,1,0:T(8,128)S(1)}) fusion(f32[1,1,16,4096]{3,2,1,0:T(8,128)S(1)} %mul.22, f32[1,1,16,4096]{3,2,1,0:T(8,128)S(1)} %copy-done, bf16[1,1,16,4096]{3,2,1,0:T(8,128)(2,1)S(1)} %copy-done.1), kind=kLoop, calls=%fused_computation.17 | loop fusion | flops 196608 | bytes 1179648 | tf_op jit(solution)/shard_map/mul | solution.py:24
  11.8 0.9 %convolution_multiply_fusion = f32[4,32,128]{2,1,0:T(8,128)} fusion(f32[4,128,128]{2,1,0:T(8,128)S(1)} %add.9, f32[4,32]{1,0:T(4,128)S(1)} %get-tuple-element.4, s32[4,32]{1,0:T(4,128)S(1)} %bitcast.20), kind=kOutput, calls=%fused_computation.1 | convolution fusion | flops 25198592 | bytes 328704 | tf_op jit(solution)/shard_map/wkb,wbc->wkc/dot_general | solution.py:26
  12.7 1.1 %all-to-all-done = f32[4,1,32]{2,1,0:T(1,128)S(1)} async-done(((f32[4,1,32]{2,1,0:T(1,128)}), f32[4,1,32]{2,1,0:T(1,128)S(1)}, u32[]{:S(2)}, u32[]{:S(2)}) %all-to-all-start) | async-done | bytes 544 | tf_op jit(solution)/shard_map/all_to_all | solution.py:32
  13.8 4.0 %all-to-all-start.1 = ((f32[4,32,128]{2,1,0:T(8,128)}), f32[4,32,128]{2,1,0:T(8,128)S(1)}, u32[]{:S(2)}, u32[]{:S(2)}) async-start(f32[4,32,128]{2,1,0:T(8,128)} %convolution_multiply_fusion), calls=%async_computation.1 | async-start | bytes 131072 | tf_op jit(solution)/shard_map/all_to_all | solution.py:31
  17.8 5.7 %all-to-all-done.1 = f32[4,32,128]{2,1,0:T(8,128)S(1)} async-done(((f32[4,32,128]{2,1,0:T(8,128)}), f32[4,32,128]{2,1,0:T(8,128)S(1)}, u32[]{:S(2)}, u32[]{:S(2)}) %all-to-all-start.1) | async-done | bytes 65568 | tf_op jit(solution)/shard_map/all_to_all | solution.py:31
  23.5 0.3 convolution_bitcast_fusion
  23.8 9.9 %all-gather = f32[1024,128]{1,0:T(8,128)S(1)} all-gather(f32[128,128]{1,0:T(8,128)S(1)} %convolution_bitcast_fusion), channel_id=2, replica_groups=mesh['grp'=8,'wide'=4] {'grp'}, dimensions={0}, use_global_device_ids=true | all-gather | bytes 589824 | tf_op jit(solution)/shard_map/all_gather | solution.py:36
  33.8 0.7 %div.10 = f32[1,4,4096]{2,1,0:T(4,128)} reshape(f32[128,128]{1,0:T(8,128)S(1)} %broadcast_multiply_fusion) | data formatting | bytes 131072 | tf_op jit(solution)/shard_map/div | solution.py:37
  (5 shorter events, 0.1 us)
Async XLA Ops:
  1.9 11.9 %all-to-all-start = ((f32[4,1,32]{2,1,0:T(1,128)}), f32[4,1,32]{2,1,0:T(1,128)S(1)}, u32[]{:S(2)}, u32[]{:S(2)}) async-start(f32[4,1,32]{2,1,0:T(1,128)} %bitcast.1), calls=%async_computation | async-start | bytes 4096 | tf_op jit(solution)/shard_map/all_to_all | solution.py:32
  8.2 0.7 %copy-start.3 = (s32[1,1,4]{2,1,0:T(1,128)S(1)}, s32[1,1,4]{2,1,0:T(1,128)}, u32[]{:S(2)}) copy-start(s32[1,1,4]{2,1,0:T(1,128)} %param.7) | copy-start | bytes 52
  9.0 0.7 %copy-start.2 = (s32[1,1,4,32]{3,2,1,0:T(4,128)S(1)}, s32[1,1,4,32]{3,2,1,0:T(4,128)}, u32[]{:S(2)}) copy-start(s32[1,1,4,32]{3,2,1,0:T(4,128)} %param.6) | copy-start | bytes 1540
  10.0 1.0 %copy-start = (f32[1,1,16,4096]{3,2,1,0:T(8,128)S(1)}, f32[1,1,16,4096]{3,2,1,0:T(8,128)}, u32[]{:S(2)}) copy-start(f32[1,1,16,4096]{3,2,1,0:T(8,128)} %param.5) | copy-start | bytes 786436
  10.0 1.0 %copy-start.1 = (bf16[1,1,16,4096]{3,2,1,0:T(8,128)(2,1)S(1)}, bf16[1,1,16,4096]{3,2,1,0:T(8,128)(2,1)}, u32[]{:S(2)}) copy-start(bf16[1,1,16,4096]{3,2,1,0:T(8,128)(2,1)} %param.4) | copy-start | bytes 393220
  13.8 9.7 %all-to-all-start.1 = ((f32[4,32,128]{2,1,0:T(8,128)}), f32[4,32,128]{2,1,0:T(8,128)S(1)}, u32[]{:S(2)}, u32[]{:S(2)}) async-start(f32[4,32,128]{2,1,0:T(8,128)} %convolution_multiply_fusion), calls=%async_computation.1 | async-start | bytes 131072 | tf_op jit(solution)/shard_map/all_to_all | solution.py:31
